TPU v7x, 512 devices: a whole 4x4x16 slice. The times are simulated.
512 devices in a mesh: row: 16 (over z), col: 16 (over y, x), layer: 2 (over core).
Axes of the slice: x: 4, y: 4, z: 16, core: 2. Of those that a mesh axis runs over, the one named last changes fastest.
Arguments:
- ratings: bfloat16 [32768, 16384], P('row', ('col', 'layer')), may hold values from -6 to 6
- tile_mask: int32 [256, 128], P('row', ('col', 'layer')), may hold values 0 or 1
- tile_counts: int32 [256, 128], P('row', ('col', 'layer')), may hold values from 1 to 16384
- user_factor: float32 [256, 32768], P(('col', 'layer'), 'row'), may hold values from -1.5 to 1.5
- item_factor: float32 [256, 16384], P('row', ('col', 'layer')), may hold values from -1.5 to 1.5
Outputs:
- new_user: float32 [256, 32768], P(('col', 'layer'), 'row')
- new_item: float32 [256, 16384], P('row', ('col', 'layer'))
- loss_value: float32 [], replicated
- grad_norm: float32 [], replicated
All inputs are finite; a program needn't handle non-finite values. No bound on the sum of `tile_mask` on one device may be relied on, other than what follows from the above.
Results may differ from a plain program's by a relative error of at most 0.0049.
Values may be sent and summed in bfloat16 or wider, within the bound.
No kernel may reach another device: no remote copies, remote signals or barrier semaphores. Data moves between devices by JAX's collectives and lax.ppermute only.
A program may use at most 64 MiB of HBM per device.

v0:
```python
import jax
import jax.numpy as jnp
from jax import lax
from jax.sharding import Mesh
from jax.sharding import PartitionSpec as P

TILE = 128
COL_LAYER = ("col_0", "col_1", "layer")
ROW_COL_LAYER = ("row", "col_0", "col_1", "layer")
epsilon = 1e-12
trust_ratio = 0.2


def from_everyone(array, axis):
    count = lax.axis_size(axis)
    return lax.all_to_all(
        jnp.broadcast_to(array[None], (count, *array.shape)), axis, 0, 0, tiled=True
    )


def joined_along(blocks, dim):
    dims = list(blocks.shape[1:])
    dims[dim] *= blocks.shape[0]
    return jnp.moveaxis(blocks, 0, dim).reshape(dims)


def gather_directly(array, axis, dim):
    blocks = from_everyone(array, axis)
    return joined_along(blocks, dim)


def by_axis(array, axes):
    for axis in axes:
        array = lax.psum(array, axis)
    return array


def in_blocks(array, dim, count):
    dims = array.shape
    blocks = array.reshape(*dims[:dim], count, dims[dim] // count, *dims[dim + 1 :])
    return jnp.moveaxis(blocks, dim, 0)


def sent_and_summed(array, axis, dim):
    blocks = in_blocks(array, dim, lax.axis_size(axis))
    arrived = lax.all_to_all(blocks, axis, split_axis=0, concat_axis=0, tiled=True)
    return arrived.astype(jnp.float32).sum(axis=0)


def tile_weights(mask_rows, count_rows):
    side = TILE
    position = lax.broadcasted_iota(jnp.int32, (side, side), 0) * side + lax.broadcasted_iota(
        jnp.int32, (side, side), 1
    )
    observed = (mask_rows[:, None, :, None] == 1) & (
        position[None, :, None, :] < count_rows[:, None, :, None]
    )
    return observed.astype(jnp.float32).reshape(
        mask_rows.shape[0] * side, mask_rows.shape[1] * side
    )


def body(ratings, tile_mask, tile_counts, user_factor, item_factor):
    user_low = user_factor.astype(jnp.bfloat16)
    item_low = item_factor.astype(jnp.bfloat16)
    user_rows = gather_directly(user_low, COL_LAYER, 0)
    item_cols = gather_directly(item_low, "row", 0)
    count_local = jnp.sum(tile_mask * tile_counts).astype(jnp.float32)
    factor_local = jnp.sum(user_factor * user_factor) + jnp.sum(item_factor * item_factor)
    predicted = lax.dot_general(
        user_rows, item_cols, (((0,), (0,)), ((), ())), preferred_element_type=jnp.float32
    )
    residual = tile_weights(tile_mask, tile_counts) * (predicted - ratings.astype(jnp.float32))
    scaled = residual.astype(jnp.bfloat16)
    error_local = jnp.sum(residual * residual)
    count_sum, factor_sum, error_sum = (
        by_axis(count_local, ROW_COL_LAYER),
        by_axis(factor_local, ROW_COL_LAYER),
        by_axis(error_local, ROW_COL_LAYER),
    )
    factor_part = user_rows
    raw_item = sent_and_summed(
        jnp.dot(factor_part, scaled, preferred_element_type=jnp.float32).astype(jnp.bfloat16),
        "row",
        0,
    )
    factor_part = item_cols
    raw_user = sent_and_summed(
        lax.dot_general(
            factor_part, scaled, (((1,), (1,)), ((), ())), preferred_element_type=jnp.float32
        ).astype(jnp.bfloat16),
        COL_LAYER,
        0,
    )
    gradient_local = jnp.sum(raw_user * raw_user) + jnp.sum(raw_item * raw_item)
    gradient_sum = by_axis(gradient_local, ROW_COL_LAYER)
    observed_total = jnp.maximum(count_sum, jnp.float32(1.0))
    loss_value = error_sum / observed_total
    grad_norm = 2.0 / observed_total * jnp.sqrt(gradient_sum + epsilon)
    factor_norm = jnp.sqrt(factor_sum + epsilon)
    rate = trust_ratio * factor_norm / grad_norm
    step_size = rate * (2.0 / observed_total)
    new_user = user_factor - step_size * raw_user
    new_item = item_factor - step_size * raw_item
    return (new_user, new_item, loss_value, grad_norm)


def solution(mesh):
    finer = Mesh(
        mesh.devices.reshape(mesh.shape["row"], 4, 4, mesh.shape["layer"]),
        ("row", "col_0", "col_1", "layer"),
    )
    return jax.shard_map(
        body,
        mesh=finer,
        in_specs=(
            P("row", COL_LAYER),
            P("row", COL_LAYER),
            P("row", COL_LAYER),
            P(COL_LAYER, "row"),
            P("row", COL_LAYER),
        ),
        out_specs=(P(COL_LAYER, "row"), P("row", COL_LAYER), P(), P()),
        check_vma=False,
    )
```

profile of v0, /device:TPU:1, one launch (start us, length us, event | category | flops | bytes accessed | tf_op | source)
XLA Modules:
  0.0 176.2 jit_solution(6132000480755298234)
XLA Ops:
  0.7 1.4 multiply_reduce_fusion.4
  2.1 0.7 broadcast_in_dim.5
  2.8 15.7 %all-to-all-start.1 = ((bf16[16,16,512]{2,1,0:T(8,128)(2,1)}), bf16[16,16,512]{2,1,0:T(8,128)(2,1)S(1)}, u32[]{:S(2)}, u32[]{:S(2)}) async-start(bf16[16,16,512]{2,1,0:T(8,128)(2,1)} %broadcast_in_dim.5), calls=%async_computation.1 | async-start | bytes 524288 | tf_op jit(solution)/shard_map/all_to_all | solution.py:16
  18.6 1.5 multiply_reduce_fusion.2
  20.1 12.2 %all-to-all-done.1 = bf16[16,16,512]{2,1,0:T(8,128)(2,1)S(1)} async-done(((bf16[16,16,512]{2,1,0:T(8,128)(2,1)}), bf16[16,16,512]{2,1,0:T(8,128)(2,1)S(1)}, u32[]{:S(2)}, u32[]{:S(2)}) %all-to-all-start.1) | async-done | bytes 262176 | tf_op jit(solution)/shard_map/all_to_all | solution.py:16
  32.3 1.1 broadcast_in_dim.4
  33.4 12.6 %all-to-all-start = ((bf16[32,8,2048]{2,1,0:T(8,128)(2,1)}), bf16[32,8,2048]{2,1,0:T(8,128)(2,1)S(1)}, u32[]{:S(2)}, u32[]{:S(2)}) async-start(bf16[32,8,2048]{2,1,0:T(8,128)(2,1)} %broadcast_in_dim.4), calls=%async_computation | async-start | bytes 2097152 | tf_op jit(solution)/shard_map/all_to_all | solution.py:16
  46.4 1.4 compare_and_fusion
  47.9 15.3 %all-to-all-done = bf16[32,8,2048]{2,1,0:T(8,128)(2,1)S(1)} async-done(((bf16[32,8,2048]{2,1,0:T(8,128)(2,1)}), bf16[32,8,2048]{2,1,0:T(8,128)(2,1)S(1)}, u32[]{:S(2)}, u32[]{:S(2)}) %all-to-all-start) | async-done | bytes 1048608 | tf_op jit(solution)/shard_map/all_to_all | solution.py:16
  63.1 4.1 %multiply_reduce_fusion = (f32[]{:T(128)}, bf16[2048,512]{1,0:T(8,128)(2,1)S(1)}) fusion(bf16[2048,512]{1,0:T(8,128)(2,1)} %param.5, bf16[256,512]{1,0:T(8,128)(2,1)S(1)} %bitcast.24, bf16[32,8,2048]{2,1,0:T(8,128)(2,1)S(1)} %all-to-all-done, pred[256,8,4,128]{3,2,1,0:T(4,128)(4,1)S(1)} %bitcast.23), kind=kOutput, calls=%fused_computation | convolution fusion | flops 543162368 | bytes 6553604 | tf_op jit(solution)/shard_map/dot_general | solution.py:70
  67.3 1.4 convolution_convert_fusion.1
  68.7 5.5 %all-to-all-start.3 = ((bf16[16,16,512]{2,1,0:T(8,128)(2,1)}), bf16[16,16,512]{2,1,0:T(8,128)(2,1)S(1)}, u32[]{:S(2)}, u32[]{:S(2)}) async-start(bf16[16,16,512]{2,1,0:T(8,128)(2,1)} %bitcast.5), calls=%async_computation.3 | async-start | bytes 524288 | tf_op jit(solution)/shard_map/all_to_all | solution.py:46
  74.2 3.3 %fusion = bf16[32,8,2048]{2,1,0:T(8,128)(2,1)} fusion(bf16[256,512]{1,0:T(8,128)(2,1)S(1)} %bitcast.25, bf16[2048,512]{1,0:T(8,128)(2,1)} %copy-done.4), kind=kOutput, calls=%fused_computation.4 | convolution fusion | flops 537395200 | bytes 3407872 | tf_op jit(solution)/shard_map/dot_general | solution.py:89
  77.5 10.7 %all-to-all-done.3 = bf16[16,16,512]{2,1,0:T(8,128)(2,1)S(1)} async-done(((bf16[16,16,512]{2,1,0:T(8,128)(2,1)}), bf16[16,16,512]{2,1,0:T(8,128)(2,1)S(1)}, u32[]{:S(2)}, u32[]{:S(2)}) %all-to-all-start.3) | async-done | bytes 262176 | tf_op jit(solution)/shard_map/all_to_all | solution.py:46
  88.2 8.8 %all-to-all-start.2 = ((bf16[32,8,2048]{2,1,0:T(8,128)(2,1)}), bf16[32,8,2048]{2,1,0:T(8,128)(2,1)S(1)}, u32[]{:S(2)}, u32[]{:S(2)}) async-start(bf16[32,8,2048]{2,1,0:T(8,128)(2,1)} %fusion), calls=%async_computation.2 | async-start | bytes 2097152 | tf_op jit(solution)/shard_map/all_to_all | solution.py:46
  97.0 0.6 multiply_reduce_fusion.5
  100.2 13.9 %all-to-all-done.2 = bf16[32,8,2048]{2,1,0:T(8,128)(2,1)S(1)} async-done(((bf16[32,8,2048]{2,1,0:T(8,128)(2,1)}), bf16[32,8,2048]{2,1,0:T(8,128)(2,1)S(1)}, u32[]{:S(2)}, u32[]{:S(2)}) %all-to-all-start.2) | async-done | bytes 1048608 | tf_op jit(solution)/shard_map/all_to_all | solution.py:46
  114.2 0.6 multiply_reduce_fusion.1
  116.2 24.6 %all-reduce = (f32[]{:T(128)}, f32[]{:T(128)}, f32[]{:T(128)}, f32[]{:T(128)}) all-reduce(f32[]{:T(128)S(6)} %add.51, f32[]{:T(128)S(6)} %convert_element_type.35, f32[]{:T(128)S(6)} %add.54, f32[]{:T(128)} %get-tuple-element.24), channel_id=1, replica_groups=mesh['row'=16,'col_0'=4,'col_1'=4,'layer'=2] {'row'}, use_global_device_ids=true, to_apply=%region_2.0 | all-reduce | flops 4 | bytes 32 | tf_op jit(solution)/shard_map/psum | solution.py:34
  140.8 7.1 %all-reduce.2 = (f32[]{:T(128)}, f32[]{:T(128)}, f32[]{:T(128)}, f32[]{:T(128)}) all-reduce(f32[]{:T(128)} %get-tuple-element.4, f32[]{:T(128)} %get-tuple-element.5, f32[]{:T(128)} %get-tuple-element.6, f32[]{:T(128)} %get-tuple-element.7), channel_id=1, replica_groups=mesh['row'=16,'col_0'=4,'col_1'=4,'layer'=2] {'col_0'}, use_global_device_ids=true, to_apply=%region_3.0 | all-reduce | flops 4 | bytes 32 | tf_op jit(solution)/shard_map/psum | solution.py:34
  147.9 8.6 %all-reduce.1 = (f32[]{:T(128)}, f32[]{:T(128)}, f32[]{:T(128)}, f32[]{:T(128)}) all-reduce(f32[]{:T(128)} %get-tuple-element.12, f32[]{:T(128)} %get-tuple-element.13, f32[]{:T(128)} %get-tuple-element.14, f32[]{:T(128)} %get-tuple-element.15), channel_id=1, replica_groups=mesh['row'=16,'col_0'=4,'col_1'=4,'layer'=2] {'col_1'}, use_global_device_ids=true, to_apply=%region_4.0 | all-reduce | flops 4 | bytes 32 | tf_op jit(solution)/shard_map/psum | solution.py:34
  156.5 13.3 %all-reduce.3 = (f32[]{:T(128)}, f32[]{:T(128)}, f32[]{:T(128)}, f32[]{:T(128)}) all-reduce(f32[]{:T(128)} %get-tuple-element.8, f32[]{:T(128)} %get-tuple-element.9, f32[]{:T(128)} %get-tuple-element.10, f32[]{:T(128)} %get-tuple-element.11), channel_id=1, replica_groups=mesh['row'=16,'col_0'=4,'col_1'=4,'layer'=2] {'layer'}, use_global_device_ids=true, to_apply=%region_5.0 | all-reduce | flops 4 | bytes 32 | tf_op jit(solution)/shard_map/psum | solution.py:34
  171.9 0.6 multiply_subtract_fusion.1
  172.6 0.6 multiply_subtract_fusion
  (18 shorter events, 1.1 us)
Async XLA Ops:
  0.6 45.5 %copy-start.3 = (s32[16,4]{0,1:T(4,128)S(1)}, s32[16,4]{0,1:T(4,128)}, u32[]{:S(2)}) copy-start(s32[16,4]{0,1:T(4,128)} %param.6) | copy-start | bytes 772
  0.6 45.6 %copy-start.2 = (s32[16,4]{0,1:T(4,128)S(1)}, s32[16,4]{0,1:T(4,128)}, u32[]{:S(2)}) copy-start(s32[16,4]{0,1:T(4,128)} %param.7) | copy-start | bytes 772
  2.8 29.5 %all-to-all-start.1 = ((bf16[16,16,512]{2,1,0:T(8,128)(2,1)}), bf16[16,16,512]{2,1,0:T(8,128)(2,1)S(1)}, u32[]{:S(2)}, u32[]{:S(2)}) async-start(bf16[16,16,512]{2,1,0:T(8,128)(2,1)} %broadcast_in_dim.5), calls=%async_computation.1 | async-start | bytes 524288 | tf_op jit(solution)/shard_map/all_to_all | solution.py:16
  33.4 29.7 %all-to-all-start = ((bf16[32,8,2048]{2,1,0:T(8,128)(2,1)}), bf16[32,8,2048]{2,1,0:T(8,128)(2,1)S(1)}, u32[]{:S(2)}, u32[]{:S(2)}) async-start(bf16[32,8,2048]{2,1,0:T(8,128)(2,1)} %broadcast_in_dim.4), calls=%async_computation | async-start | bytes 2097152 | tf_op jit(solution)/shard_map/all_to_all | solution.py:16
  67.3 1.4 copy-start.4
  68.7 19.5 %all-to-all-start.3 = ((bf16[16,16,512]{2,1,0:T(8,128)(2,1)}), bf16[16,16,512]{2,1,0:T(8,128)(2,1)S(1)}, u32[]{:S(2)}, u32[]{:S(2)}) async-start(bf16[16,16,512]{2,1,0:T(8,128)(2,1)} %bitcast.5), calls=%async_computation.3 | async-start | bytes 524288 | tf_op jit(solution)/shard_map/all_to_all | solution.py:46
  77.5 94.4 %copy-start.1 = (f32[16,512]{1,0:T(8,128)S(1)}, f32[16,512]{1,0:T(8,128)}, u32[]{:S(2)}) copy-start(f32[16,512]{1,0:T(8,128)} %param.9) | copy-start | bytes 98308
  77.5 95.0 %copy-start = (f32[8,2048]{1,0:T(8,128)S(1)}, f32[8,2048]{1,0:T(8,128)}, u32[]{:S(2)}) copy-start(f32[8,2048]{1,0:T(8,128)} %param.8) | copy-start | bytes 196612
  88.2 25.9 %all-to-all-start.2 = ((bf16[32,8,2048]{2,1,0:T(8,128)(2,1)}), bf16[32,8,2048]{2,1,0:T(8,128)(2,1)S(1)}, u32[]{:S(2)}, u32[]{:S(2)}) async-start(bf16[32,8,2048]{2,1,0:T(8,128)(2,1)} %fusion), calls=%async_computation.2 | async-start | bytes 2097152 | tf_op jit(solution)/shard_map/all_to_all | solution.py:46
where the time goes:
time: 177 us; the launch traced here: 176 us
  blocking collectives  53.6 us (30%)
  waiting for transfers between devices  52.1 us (29%)
  starting transfers between devices  42.6 us (24%)
  between operations  9.06 us (5%)
  matrix products  8.87 us (5%)
  other arithmetic  7.83 us (4%)
  local copies, waits for them, and re-layouts  2.03 us (1%)
    psum x4, blocking collectives, by_axis(): array = lax.psum(array, axis)  53.6 us
    all_to_all x2, starting transfers between devices, from_everyone(): lax.all_to_all(jnp.broadcast_to(array[None], (count, *array.shape)), axis...  28.4 us
    all_to_all x2, waiting for transfers between devices, from_everyone(): lax.all_to_all(jnp.broadcast_to(array[None], (count, *array.shape)), axis...  27.5 us
    all_to_all x2, waiting for transfers between devices, sent_and_summed(): lax.all_to_all(blocks, axis, split_axis=0, concat_axis=0, tiled=True)  24.6 us
    all_to_all x2, starting transfers between devices, sent_and_summed(): lax.all_to_all(blocks, axis, split_axis=0, concat_axis=0, tiled=True)  14.3 us
    dot_general x1, matrix products, body(): lax.dot_general(user_rows, item_cols, (((0,), (0,)), ((), ())), preferred...  4.12 us
  transfers between devices with their start and end apart: 4, of which 4 were waited for; matrix products, arithmetic and copies ran while one was open for 4% of the time, Pallas kernels for 0%

commit v1 on v0

--- a/solution.py
+++ b/solution.py
@@ -31,7 +31,7 @@
 
 def by_axis(array, axes):
     for axis in axes:
-        array = lax.psum(array, axis)
+        array = jnp.sum(lax.all_gather(array, axis), axis=0)
     return array
 
 

time: 177 us -> 205 us (1.16)
  local copies, waits for them, and re-layouts: 2.03 us -> 28.5 us
  other arithmetic: 7.83 us -> 17.4 us
  waiting for transfers between devices: 52.1 us -> 45.8 us
  blocking collectives: 53.6 us -> 51 us
    psum x4 -> x0, blocking collectives: 53.6 us -> none  [by_axis(): array = lax.psum(array, axis)]
    unnamed x0 -> x4, blocking collectives: none -> 51 us
    unnamed x11 -> x47, local copies, waits for them, and re-layouts: 0.1 us -> 26.6 us
    reduce_sum x0 -> x16, other arithmetic: none -> 9.61 us  [by_axis(): array = jnp.sum(lax.all_gather(array, axis), axis=0)]
    all_to_all x2, waiting for transfers between devices: 24.6 us -> 19 us  [sent_and_summed(): lax.all_to_all(blocks, axis, split_axis=0, concat_axis=0, tiled=True)]
  transfers between devices with their start and end apart: 4 -> 4, of which waited for: 4 -> 4; matrix products, arithmetic and copies ran while one was open for 4% -> 7% of each run, Pallas kernels for 0% -> 0%
where the time goes in v1:
time: 205 us; the launch traced here: 203 us
  blocking collectives  51 us (25%)
  waiting for transfers between devices  45.8 us (22%)
  starting transfers between devices  42.6 us (21%)
  local copies, waits for them, and re-layouts  28.5 us (14%)
  other arithmetic  17.4 us (8%)
  between operations  9.08 us (4%)
  matrix products  8.84 us (4%)
    unnamed x4, blocking collectives  51 us
    all_to_all x2, starting transfers between devices, from_everyone(): lax.all_to_all(jnp.broadcast_to(array[None], (count, *array.shape)), axis...  28.4 us
    all_to_all x2, waiting for transfers between devices, from_everyone(): lax.all_to_all(jnp.broadcast_to(array[None], (count, *array.shape)), axis...  26.9 us
    unnamed x47, local copies, waits for them, and re-layouts  26.6 us
    all_to_all x2, waiting for transfers between devices, sent_and_summed(): lax.all_to_all(blocks, axis, split_axis=0, concat_axis=0, tiled=True)  19 us
    all_to_all x2, starting transfers between devices, sent_and_summed(): lax.all_to_all(blocks, axis, split_axis=0, concat_axis=0, tiled=True)  14.3 us
    reduce_sum x16, other arithmetic, by_axis(): array = jnp.sum(lax.all_gather(array, axis), axis=0)  9.61 us
  transfers between devices with their start and end apart: 4, of which 4 were waited for; matrix products, arithmetic and copies ran while one was open for 7% of the time, Pallas kernels for 0%

profile of v1, /device:TPU:1, one launch (start us, length us, event | category | flops | bytes accessed | tf_op | source)
XLA Modules:
  0.0 203.3 jit_solution(6204629614202432438)
XLA Ops:
  0.6 1.4 multiply_reduce_fusion.4
  2.8 15.7 %all-to-all-start.1 = ((bf16[16,16,512]{2,1,0:T(8,128)(2,1)}), bf16[16,16,512]{2,1,0:T(8,128)(2,1)S(1)}, u32[]{:S(2)}, u32[]{:S(2)}) async-start(bf16[16,16,512]{2,1,0:T(8,128)(2,1)} %broadcast_in_dim.5), calls=%async_computation.1 | async-start | bytes 524288 | tf_op jit(solution)/shard_map/all_to_all | solution.py:16
  19.3 1.5 multiply_reduce_fusion.2
  20.8 11.5 %all-to-all-done.1 = bf16[16,16,512]{2,1,0:T(8,128)(2,1)S(1)} async-done(((bf16[16,16,512]{2,1,0:T(8,128)(2,1)}), bf16[16,16,512]{2,1,0:T(8,128)(2,1)S(1)}, u32[]{:S(2)}, u32[]{:S(2)}) %all-to-all-start.1) | async-done | bytes 262176 | tf_op jit(solution)/shard_map/all_to_all | solution.py:16
  33.4 12.6 %all-to-all-start = ((bf16[32,8,2048]{2,1,0:T(8,128)(2,1)}), bf16[32,8,2048]{2,1,0:T(8,128)(2,1)S(1)}, u32[]{:S(2)}, u32[]{:S(2)}) async-start(bf16[32,8,2048]{2,1,0:T(8,128)(2,1)} %broadcast_in_dim.4), calls=%async_computation | async-start | bytes 2097152 | tf_op jit(solution)/shard_map/all_to_all | solution.py:16
  46.3 1.4 compare_and_fusion
  47.8 15.4 %all-to-all-done = bf16[32,8,2048]{2,1,0:T(8,128)(2,1)S(1)} async-done(((bf16[32,8,2048]{2,1,0:T(8,128)(2,1)}), bf16[32,8,2048]{2,1,0:T(8,128)(2,1)S(1)}, u32[]{:S(2)}, u32[]{:S(2)}) %all-to-all-start) | async-done | bytes 1048608 | tf_op jit(solution)/shard_map/all_to_all | solution.py:16
  63.1 4.1 %multiply_reduce_fusion = (f32[]{:T(128)}, bf16[2048,512]{1,0:T(8,128)(2,1)S(1)}) fusion(bf16[2048,512]{1,0:T(8,128)(2,1)} %param.5, bf16[256,512]{1,0:T(8,128)(2,1)S(1)} %bitcast.44, bf16[32,8,2048]{2,1,0:T(8,128)(2,1)S(1)} %all-to-all-done, pred[256,8,4,128]{3,2,1,0:T(4,128)(4,1)S(1)} %bitcast.43), kind=kOutput, calls=%fused_computation | convolution fusion | flops 543162368 | bytes 6553604 | tf_op jit(solution)/shard_map/dot_general | solution.py:70
  67.2 1.4 convolution_convert_fusion.1
  68.7 5.5 %all-to-all-start.3 = ((bf16[16,16,512]{2,1,0:T(8,128)(2,1)}), bf16[16,16,512]{2,1,0:T(8,128)(2,1)S(1)}, u32[]{:S(2)}, u32[]{:S(2)}) async-start(bf16[16,16,512]{2,1,0:T(8,128)(2,1)} %bitcast.17), calls=%async_computation.3 | async-start | bytes 524288 | tf_op jit(solution)/shard_map/all_to_all | solution.py:46
  74.2 3.3 %fusion = bf16[32,8,2048]{2,1,0:T(8,128)(2,1)} fusion(bf16[256,512]{1,0:T(8,128)(2,1)S(1)} %bitcast.45, bf16[2048,512]{1,0:T(8,128)(2,1)} %copy-done.4), kind=kOutput, calls=%fused_computation.4 | convolution fusion | flops 537395200 | bytes 3407872 | tf_op jit(solution)/shard_map/dot_general | solution.py:89
  77.5 10.7 %all-to-all-done.3 = bf16[16,16,512]{2,1,0:T(8,128)(2,1)S(1)} async-done(((bf16[16,16,512]{2,1,0:T(8,128)(2,1)}), bf16[16,16,512]{2,1,0:T(8,128)(2,1)S(1)}, u32[]{:S(2)}, u32[]{:S(2)}) %all-to-all-start.3) | async-done | bytes 262176 | tf_op jit(solution)/shard_map/all_to_all | solution.py:46
  88.2 8.8 %all-to-all-start.2 = ((bf16[32,8,2048]{2,1,0:T(8,128)(2,1)}), bf16[32,8,2048]{2,1,0:T(8,128)(2,1)S(1)}, u32[]{:S(2)}, u32[]{:S(2)}) async-start(bf16[32,8,2048]{2,1,0:T(8,128)(2,1)} %fusion), calls=%async_computation.2 | async-start | bytes 2097152 | tf_op jit(solution)/shard_map/all_to_all | solution.py:46
  103.7 1.4 dynamic-update-slice.12
  105.7 8.3 %all-to-all-done.2 = bf16[32,8,2048]{2,1,0:T(8,128)(2,1)S(1)} async-done(((bf16[32,8,2048]{2,1,0:T(8,128)(2,1)}), bf16[32,8,2048]{2,1,0:T(8,128)(2,1)S(1)}, u32[]{:S(2)}, u32[]{:S(2)}) %all-to-all-start.2) | async-done | bytes 1048608 | tf_op jit(solution)/shard_map/all_to_all | solution.py:46
  116.9 23.9 %all-reduce.16 = (f32[16]{0:T(128)S(1)}, f32[16]{0:T(128)S(1)}, f32[16]{0:T(128)S(1)}, f32[16]{0:T(128)S(1)}) all-reduce(f32[16]{0:T(128)S(1)} %dynamic-update-slice, f32[16]{0:T(128)S(1)} %dynamic-update-slice.4, f32[16]{0:T(128)S(1)} %dynamic-update-slice.8, ...), channel_id=1, replica_groups=mesh['row'=16,'col_0'=4,'col_1'=4,'layer'=2] {'row'}, use_global_device_ids=true, to_apply=%add | all-reduce | flops 64 | bytes 512
  142.0 1.4 dynamic-update-slice.13
  143.5 1.4 dynamic-update-slice.9
  145.5 1.4 dynamic-update-slice.5
  147.6 1.4 dynamic-update-slice.1
  150.3 6.5 %all-reduce.18 = (f32[4]{0:T(128)S(1)}, f32[4]{0:T(128)S(1)}, f32[4]{0:T(128)S(1)}, f32[4]{0:T(128)S(1)}) all-reduce(f32[4]{0:T(128)S(1)} %dynamic-update-slice.1, f32[4]{0:T(128)S(1)} %dynamic-update-slice.5, f32[4]{0:T(128)S(1)} %dynamic-update-slice.9, ...), channel_id=1, replica_groups=mesh['row'=16,'col_0'=4,'col_1'=4,'layer'=2] {'col_0'}, use_global_device_ids=true, to_apply=%add.1 | all-reduce | flops 16 | bytes 128
  159.4 1.4 dynamic-update-slice.14
  166.0 7.9 %all-reduce.17 = (f32[4]{0:T(128)S(1)}, f32[4]{0:T(128)S(1)}, f32[4]{0:T(128)S(1)}, f32[4]{0:T(128)S(1)}) all-reduce(f32[4]{0:T(128)S(1)} %dynamic-update-slice.2, f32[4]{0:T(128)S(1)} %dynamic-update-slice.6, f32[4]{0:T(128)S(1)} %dynamic-update-slice.10, ...), channel_id=1, replica_groups=mesh['row'=16,'col_0'=4,'col_1'=4,'layer'=2] {'col_1'}, use_global_device_ids=true, to_apply=%add.2 | all-reduce | flops 16 | bytes 128
  182.0 12.6 %all-reduce.19 = (f32[2]{0:T(128)S(1)}, f32[2]{0:T(128)S(1)}, f32[2]{0:T(128)S(1)}, f32[2]{0:T(128)S(1)}) all-reduce(f32[2]{0:T(128)S(1)} %dynamic-update-slice.3, f32[2]{0:T(128)S(1)} %dynamic-update-slice.7, f32[2]{0:T(128)S(1)} %dynamic-update-slice.11, ...), channel_id=1, replica_groups=mesh['row'=16,'col_0'=4,'col_1'=4,'layer'=2] {'layer'}, use_global_device_ids=true, to_apply=%add.3 | all-reduce | flops 8 | bytes 64
  (70 shorter events, 33.0 us)
Async XLA Ops:
  0.6 45.5 %copy-start.3 = (s32[16,4]{0,1:T(4,128)S(1)}, s32[16,4]{0,1:T(4,128)}, u32[]{:S(2)}) copy-start(s32[16,4]{0,1:T(4,128)} %param.6) | copy-start | bytes 772
  2.8 29.5 %all-to-all-start.1 = ((bf16[16,16,512]{2,1,0:T(8,128)(2,1)}), bf16[16,16,512]{2,1,0:T(8,128)(2,1)S(1)}, u32[]{:S(2)}, u32[]{:S(2)}) async-start(bf16[16,16,512]{2,1,0:T(8,128)(2,1)} %broadcast_in_dim.5), calls=%async_computation.1 | async-start | bytes 524288 | tf_op jit(solution)/shard_map/all_to_all | solution.py:16
  33.4 29.7 %all-to-all-start = ((bf16[32,8,2048]{2,1,0:T(8,128)(2,1)}), bf16[32,8,2048]{2,1,0:T(8,128)(2,1)S(1)}, u32[]{:S(2)}, u32[]{:S(2)}) async-start(bf16[32,8,2048]{2,1,0:T(8,128)(2,1)} %broadcast_in_dim.4), calls=%async_computation | async-start | bytes 2097152 | tf_op jit(solution)/shard_map/all_to_all | solution.py:16
  67.2 1.4 copy-start.4
  68.7 19.5 %all-to-all-start.3 = ((bf16[16,16,512]{2,1,0:T(8,128)(2,1)}), bf16[16,16,512]{2,1,0:T(8,128)(2,1)S(1)}, u32[]{:S(2)}, u32[]{:S(2)}) async-start(bf16[16,16,512]{2,1,0:T(8,128)(2,1)} %bitcast.17), calls=%async_computation.3 | async-start | bytes 524288 | tf_op jit(solution)/shard_map/all_to_all | solution.py:46
  77.5 19.5 %copy-start.2 = (s32[16,4]{0,1:T(4,128)S(1)}, s32[16,4]{0,1:T(4,128)}, u32[]{:S(2)}) copy-start(s32[16,4]{0,1:T(4,128)} %param.7) | copy-start | bytes 772
  77.5 121.1 %copy-start.1 = (f32[16,512]{1,0:T(8,128)S(1)}, f32[16,512]{1,0:T(8,128)}, u32[]{:S(2)}) copy-start(f32[16,512]{1,0:T(8,128)} %param.9) | copy-start | bytes 98308
  77.5 121.7 %copy-start = (f32[8,2048]{1,0:T(8,128)S(1)}, f32[8,2048]{1,0:T(8,128)}, u32[]{:S(2)}) copy-start(f32[8,2048]{1,0:T(8,128)} %param.8) | copy-start | bytes 196612
  88.2 25.9 %all-to-all-start.2 = ((bf16[32,8,2048]{2,1,0:T(8,128)(2,1)}), bf16[32,8,2048]{2,1,0:T(8,128)(2,1)S(1)}, u32[]{:S(2)}, u32[]{:S(2)}) async-start(bf16[32,8,2048]{2,1,0:T(8,128)(2,1)} %fusion), calls=%async_computation.2 | async-start | bytes 2097152 | tf_op jit(solution)/shard_map/all_to_all | solution.py:46
